TPU v7x, 32 devices: a whole 2x2x4 slice. The times are simulated.
32 devices in a mesh: group: 4 (over z), dom: 8 (over y, x, core).
Axes of the slice: x: 2, y: 2, z: 4, core: 2. Of those that a mesh axis runs over, the one named last changes fastest.
Arguments:
- features: bfloat16 [16384, 128], P(('group', 'dom')), may hold values from -6 to 6
- cotangent: bfloat16 [16384, 128], P(('group', 'dom')), may hold values from -6 to 6
- fine_send: int32 [256, 16], P(('group', 'dom')), may hold values from 0 to 512, as said below
- fine_rim: int32 [64, 128], P(('group', 'dom')), may hold values from 0 to 511
- fine_src: int32 [131072], P(('group', 'dom')), may hold values from 0 to 895, as said below
- fine_dst: int32 [131072], P(('group', 'dom')), may hold values from 0 to 511
- fine_pool: int32 [16384], P(('group', 'dom')), may hold values from 0 to 255, as said below
- coarse_send: int32 [256, 4], P(('group', 'dom')), may hold values from 0 to 32, as said below
- coarse_src: int32 [8192], P(('group', 'dom')), may hold values from 0 to 63, as said below
- coarse_dst: int32 [8192], P(('group', 'dom')), may hold values from 0 to 31
- coarse_pool: int32 [1024], P(('group', 'dom')), may hold values from 0 to 511
- w_send: bfloat16 [128, 128], replicated, may hold values from -0.5 to 0.5
- w_recv: bfloat16 [128, 128], replicated, may hold values from -0.5 to 0.5
- w_node: bfloat16 [128, 128], replicated, may hold values from -0.5 to 0.5
- v_send: bfloat16 [128, 128], replicated, may hold values from -0.5 to 0.5
- v_recv: bfloat16 [128, 128], replicated, may hold values from -0.5 to 0.5
- v_node: bfloat16 [128, 128], replicated, may hold values from -0.5 to 0.5
- w_top: bfloat16 [128, 128], replicated, may hold values from -0.5 to 0.5
Outputs:
- flow: bfloat16 [16384, 128], P(('group', 'dom'))
- grad_features: float32 [16384, 128], P(('group', 'dom'))
- grad_send: float32 [128, 128], replicated
Inputs may be any that keep to these rules, and one draw needn't show every extreme that they name: `fine_send`: each device holds 8 rows of 16: row p lists own node rows for the device with dom index p of its group; the value 512 marks an empty slot, live slots come first, and three rows of every device are full. `fine_rim`: each device holds two rows: the first go to the previous group's device of the same dom index, the second to the next group's. `fine_src`: index into the device's extended rows: its 512 nodes, 128 rows from its group in dom order, 128 rows from the previous group, 128 from the next. `fine_pool`: coarse node numbered within the node's group. `coarse_send`: as fine_send with 4 slots a row and 32 marking an empty slot. `coarse_src`: index into the device's coarse rows, then 8 * 4 rows from its group in dom order.
All inputs are finite; a program needn't handle non-finite values.
Results may differ from a plain program's by a relative error of at most 0.025.
Values may be sent and summed in bfloat16 or wider, within the bound.
No kernel may reach another device: no remote copies, remote signals or barrier semaphores. Data moves between devices by JAX's collectives and lax.ppermute only.
A program may use at most 64 MiB of HBM per device.

v0:
```python
import jax
import jax.numpy as jnp
from jax import lax
from jax.sharding import PartitionSpec as P

NCC = 512


def with_halo(block, sides, width):
    for axis, dim in sides:
        count = lax.axis_size(axis)
        forward = [(i, i + 1) for i in range(count - 1)]
        backward = [(target, source) for source, target in forward]
        low = lax.ppermute(
            lax.slice_in_dim(block, block.shape[dim] - width, None, axis=dim), axis, forward
        )
        high = lax.ppermute(lax.slice_in_dim(block, 0, width, axis=dim), axis, backward)
        block = jnp.concatenate([low, block, high], axis=dim)
    return block


def silu_slope(values):
    sigma = jax.nn.sigmoid(values)
    return sigma * (1.0 + values * (1.0 - sigma))


def edge_forward(extended, own_rows, sources, targets, w_send, w_recv, w_node):
    preact = jnp.dot(extended[sources], w_send, preferred_element_type=jnp.float32)
    preact = preact + jnp.dot(own_rows[targets], w_recv, preferred_element_type=jnp.float32)
    message = jax.nn.silu(preact).astype(jnp.bfloat16)
    summed = jax.ops.segment_sum(
        message.astype(jnp.float32), targets, num_segments=own_rows.shape[0]
    ).astype(jnp.bfloat16)
    updated = (
        own_rows.astype(jnp.float32) + jnp.dot(summed, w_node, preferred_element_type=jnp.float32)
    ).astype(jnp.bfloat16)
    return (updated, preact)


def edge_backward(grad_out, extended, own_rows, preact, sources, targets, w_send, w_recv, w_node):
    rounded = grad_out.astype(jnp.bfloat16)
    grad_sum = jnp.dot(rounded, w_node.T, preferred_element_type=jnp.float32)
    grad_pre = (grad_sum[targets] * silu_slope(preact)).astype(jnp.bfloat16)
    grad_ext = jax.ops.segment_sum(
        jnp.dot(grad_pre, w_send.T, preferred_element_type=jnp.float32),
        sources,
        num_segments=extended.shape[0],
    )
    own_count = own_rows.shape[0]
    grad_own = grad_out + jax.ops.segment_sum(
        jnp.dot(grad_pre, w_recv.T, preferred_element_type=jnp.float32),
        targets,
        num_segments=own_count,
    )
    grad_own = grad_own + grad_ext[:own_count]
    grad_weight = lax.dot_general(
        extended[sources], grad_pre, (((0,), (0,)), ((), ())), preferred_element_type=jnp.float32
    )
    return (grad_own, grad_ext[own_count:], grad_weight)


def top_forward(pooled, w_top):
    slope_in = jnp.dot(pooled.astype(jnp.bfloat16), w_top, preferred_element_type=jnp.float32)
    return ((pooled + jax.nn.silu(slope_in)).astype(jnp.bfloat16), slope_in)


def top_backward(grad_top, slope_in, w_top):
    inner = (grad_top * silu_slope(slope_in)).astype(jnp.bfloat16)
    return grad_top + jnp.dot(inner, w_top.T, preferred_element_type=jnp.float32)


def add_rows(grads, index, values):
    padded = jnp.concatenate([grads, jnp.zeros((1, grads.shape[1]), jnp.float32)], axis=0)
    return padded.at[index].add(values)[:-1]


def local(
    features,
    cotangent,
    fine_send,
    fine_rim,
    fine_src,
    fine_dst,
    fine_pool,
    coarse_send,
    coarse_src,
    coarse_dst,
    coarse_pool,
    w_send,
    w_recv,
    w_node,
    v_send,
    v_recv,
    v_node,
    w_top,
):
    width = features.shape[1]
    dom_count = lax.axis_size("dom")
    coarse_count = coarse_pool.shape[0]
    group_coarse = coarse_count * dom_count
    slot_rows = fine_send.shape[1]
    coarse_slots = coarse_send.shape[1]
    rim_count = fine_rim.shape[1]
    padded = jnp.concatenate([features, jnp.zeros((1, width), jnp.bfloat16)], axis=0)
    incoming = lax.all_to_all(
        padded[fine_send], "dom", split_axis=0, concat_axis=0, tiled=True
    ).reshape(-1, width)
    rim_rows = with_halo(features[fine_rim], (("group", 0),), 1)
    extended = jnp.concatenate([features, incoming, rim_rows[0], rim_rows[3]], axis=0)
    updated, preact = edge_forward(extended, features, fine_src, fine_dst, w_send, w_recv, w_node)
    partial_value = jax.ops.segment_sum(
        updated.astype(jnp.float32), fine_pool, num_segments=group_coarse
    )
    grad_flow = cotangent.astype(jnp.float32)
    grad_partial = jax.ops.segment_sum(grad_flow, fine_pool, num_segments=group_coarse)
    owned = lax.psum_scatter(partial_value, "dom", scatter_dimension=0, tiled=True)
    grad_coarse = lax.psum_scatter(grad_partial, "dom", scatter_dimension=0, tiled=True)
    coarse_in = (0.25 * owned).astype(jnp.bfloat16)
    cpadded = jnp.concatenate([coarse_in, jnp.zeros((1, width), jnp.bfloat16)], axis=0)
    cincoming = lax.all_to_all(
        cpadded[coarse_send], "dom", split_axis=0, concat_axis=0, tiled=True
    ).reshape(-1, width)
    cextended = jnp.concatenate([coarse_in, cincoming], axis=0)
    coarse_mid, cpreact = edge_forward(
        cextended, coarse_in, coarse_src, coarse_dst, v_send, v_recv, v_node
    )
    top_partial = jax.ops.segment_sum(coarse_mid.astype(jnp.float32), coarse_pool, num_segments=NCC)
    grad_top_partial = jax.ops.segment_sum(grad_coarse, coarse_pool, num_segments=NCC)
    top_total = lax.psum(top_partial, ("group", "dom"))
    grad_top = lax.psum(grad_top_partial, ("group", "dom"))
    pooled = 0.125 * top_total
    top_out, slope_in = top_forward(pooled, w_top)
    coarse_out = (coarse_mid.astype(jnp.float32) + top_out[coarse_pool].astype(jnp.float32)).astype(
        jnp.bfloat16
    )
    coarse_table = lax.all_gather(coarse_out, "dom", axis=0, tiled=True)
    flow = (updated.astype(jnp.float32) + coarse_table[fine_pool].astype(jnp.float32)).astype(
        jnp.bfloat16
    )
    grad_pool = top_backward(grad_top, slope_in, w_top)
    grad_cmid = grad_coarse + 0.125 * grad_pool[coarse_pool]
    c_own, c_halo, c_weight = edge_backward(
        grad_cmid, cextended, coarse_in, cpreact, coarse_src, coarse_dst, v_send, v_recv, v_node
    )
    creturned = lax.all_to_all(
        c_halo.reshape(dom_count, coarse_slots, width),
        "dom",
        split_axis=0,
        concat_axis=0,
        tiled=True,
    )
    grad_cin = add_rows(c_own, coarse_send.reshape(-1), creturned.reshape(-1, width))
    grad_table = lax.all_gather(grad_cin, "dom", axis=0, tiled=True)
    grad_fmid = grad_flow + 0.25 * grad_table[fine_pool]
    f_own, f_halo, f_weight = edge_backward(
        grad_fmid, extended, features, preact, fine_src, fine_dst, w_send, w_recv, w_node
    )
    split = dom_count * slot_rows
    returned = lax.all_to_all(
        f_halo[:split].reshape(dom_count, slot_rows, width),
        "dom",
        split_axis=0,
        concat_axis=0,
        tiled=True,
    )
    grad_x = add_rows(f_own, fine_send.reshape(-1), returned.reshape(-1, width))
    rim_grads = jnp.stack([f_halo[split : split + rim_count], f_halo[split + rim_count :]], axis=0)
    rim_back = with_halo(rim_grads, (("group", 0),), 1)
    rim_values = jnp.concatenate([rim_back[0], rim_back[3]], axis=0)
    grad_x = add_rows(grad_x, fine_rim.reshape(-1), rim_values)
    grad_send = lax.psum(f_weight, ("group", "dom"))
    return (flow, grad_x, grad_send)


def solution(mesh):
    placed = (
        P(("group", "dom"), None),
        P(("group", "dom"), None),
        P(("group", "dom"), None),
        P(("group", "dom"), None),
        P(("group", "dom")),
        P(("group", "dom")),
        P(("group", "dom")),
        P(("group", "dom"), None),
        P(("group", "dom")),
        P(("group", "dom")),
        P(("group", "dom")),
        P(),
        P(),
        P(),
        P(),
        P(),
        P(),
        P(),
    )
    return jax.shard_map(
        local,
        mesh=mesh,
        in_specs=placed,
        out_specs=(P(("group", "dom"), None), P(("group", "dom"), None), P()),
        check_vma=False,
    )
```

profile of v0, /device:TPU:1, one launch (start us, length us, event | category | flops | bytes accessed | tf_op | source)
XLA Modules:
  0.0 539.3 jit_solution(17636104793602975725)
XLA Ops:
  7.9 1.6 gather_fusion.1
  9.6 1.3 collective-permute-start.1
  10.9 4.6 collective-permute-start
  17.2 1.3 gather_fusion
  18.6 5.1 all-to-all-start
  24.4 12.1 %gather_fusion.3 = bf16[4096,128]{1,0:T(8,128)(2,1)S(1)} fusion(bf16[512,128]{1,0:T(8,128)(2,1)S(1)} %copy-done.1, s32[4096]{0:T(1024)S(1)} %fusion.37), kind=kCustom, calls=%fused_computation.3 | custom fusion | bytes 2113536 | tf_op jit(solution)/shard_map/gather | solution.py:29
  36.6 1.8 fusion.52
  38.4 12.1 %gather_fusion.2 = bf16[4096,128]{1,0:T(8,128)(2,1)S(1)} fusion(bf16[896,128]{1,0:T(8,128)(2,1)S(1)} %pad_maximum_fusion, s32[4096]{0:T(1024)S(1)} %fusion.36), kind=kCustom, calls=%fused_computation.2 | custom fusion | bytes 2113536 | tf_op jit(solution)/shard_map/gather | solution.py:28
  50.5 2.0 convolution_add_fusion
  52.6 23.8 %scatter_custom_fusion = f32[512,128]{1,0:T(8,128)} fusion(s32[4096]{0:T(1024)} %param.23, f32[4096,128]{1,0:T(8,128)S(1)} %convolution_add_fusion, f32[]{:T(128)} %constant.20.clone.1, f32[]{:T(128)} %constant.14.clone.1), kind=kCustom, calls=%fused_computation.28 | custom fusion | flops 3670016 | bytes 2360320 | tf_op jit(solution)/shard_map/scatter-add | solution.py:31
  76.4 1.8 fusion.3
  78.2 3.2 scatter_custom_fusion.1
  81.5 3.0 scatter_custom_fusion.4
  84.5 1.3 compare_select_fusion.4
  91.4 23.3 %reduce-scatter.3.cloned.1.call-done = f32[32,128]{1,0:T(8,128)} async-done(((f32[256,128]{1,0:T(8,128)}), f32[32,128]{1,0:T(8,128)}) %reduce-scatter.3.cloned.1.call-update) | async-done | bytes 16400 | tf_op jit(solution)/shard_map/reduce_scatter | solution.py:116
  116.6 4.5 all-to-all-start.1
  121.6 30.2 %reduce-scatter.5.cloned.1.call-done = f32[32,128]{1,0:T(8,128)} async-done(((f32[256,128]{1,0:T(8,128)}), f32[32,128]{1,0:T(8,128)}) %reduce-scatter.5.cloned.1.call-update) | async-done | bytes 16400 | tf_op jit(solution)/shard_map/reduce_scatter | solution.py:117
  151.9 1.6 scatter_custom_fusion.5
  156.2 1.6 scatter_custom_fusion.2
  158.0 1.5 scatter_custom_fusion.3
  159.5 1.3 pad_clamp_fusion
  160.8 1.2 compare_select_fusion.3
  162.0 126.7 %all-reduce.10.cloned.1.call-done = (f32[512,128]{1,0:T(8,128)}, f32[512,128]{1,0:T(8,128)}) async-done(((f32[512,128]{1,0:T(8,128)}, f32[512,128]{1,0:T(8,128)}), (f32[512,128]{1,0:T(8,128)}, f32[512,128]{1,0:T(8,128)})) %all-reduce.10.cloned.1.call-update) | async-done | bytes 524304 | tf_op jit(solution)/shard_map/psum | solution.py:129
  288.7 1.9 add_convert_fusion.1
  291.4 10.7 %all_gather.6 = bf16[256,128]{1,0:T(8,128)(2,1)S(1)} all-gather(bf16[32,128]{1,0:T(8,128)(2,1)S(1)} %add_convert_fusion.2), channel_id=1, replica_groups=mesh['group'=4,'dom'=8] {'dom'}, dimensions={0}, use_global_device_ids=true | all-gather | bytes 73728 | tf_op jit(solution)/shard_map/all_gather | solution.py:136
  302.1 1.5 gather_fusion.8
  303.6 1.6 add_convert_fusion
  305.2 2.1 convolution_add_fusion.1
  307.3 1.6 gather_fusion.9
  309.9 1.6 gather_fusion.10
  312.6 1.6 scatter_custom_fusion.6
  314.8 3.4 all-to-all-start.2
  318.4 1.9 scatter_fusion
  320.4 1.9 all-to-all-done.2
  323.0 8.8 %all_gather.7 = f32[256,128]{1,0:T(8,128)S(1)} all-gather(f32[32,128]{1,0:T(8,128)S(1)} %slice.78), channel_id=1, replica_groups=mesh['group'=4,'dom'=8] {'dom'}, dimensions={0}, use_global_device_ids=true | all-gather | bytes 147456 | tf_op jit(solution)/shard_map/all_gather | solution.py:153
  331.9 1.6 gather_fusion.11
  334.7 14.2 %gather_fusion.12 = f32[4096,128]{1,0:T(8,128)} fusion(f32[512,128]{1,0:T(8,128)S(1)} %fusion.15, s32[4096]{0:T(1024)S(1)} %fusion.37), kind=kCustom, calls=%fused_computation.12 | custom fusion | bytes 4210688 | tf_op jit(solution)/shard_map/gather | solution.py:43
  348.9 2.4 multiply_convert_fusion
  351.2 1.8 fusion.56
  354.6 22.8 %scatter_custom_fusion.9 = f32[896,128]{1,0:T(8,128)S(1)} fusion(s32[4096]{0:T(1024)} %param.22, f32[4096,128]{1,0:T(8,128)} %fusion.56, f32[]{:T(128)} %constant.14.clone.1), kind=kCustom, calls=%fused_computation.54 | custom fusion | flops 524288 | bytes 459264 | tf_op jit(solution)/shard_map/scatter-add | solution.py:44
  378.0 3.4 all-to-all-start.3
  382.5 22.5 %scatter_fusion.2 = f32[512,128]{1,0:T(8,128)S(1)} fusion(f32[512,128]{1,0:T(8,128)S(1)} %slice_add_fusion, s32[4096]{0:T(1024)S(1)} %copy-done.10, f32[4096,128]{1,0:T(8,128)S(1)} %fusion.57), kind=kCustom, calls=%fused_computation.23 | custom fusion | flops 524288 | bytes 6307840 | tf_op jit(solution)/shard_map/scatter-add | solution.py:50
  405.0 1.3 collective-permute-start.3
  406.3 4.0 collective-permute-start.2
  410.3 1.3 scatter_fusion.3
  411.8 2.1 scatter_custom_fusion.12
  414.7 116.5 %all-reduce.8.cloned.1.call-done = f32[128,128]{1,0:T(8,128)} async-done(((f32[128,128]{1,0:T(8,128)}), f32[128,128]{1,0:T(8,128)}) %all-reduce.8.cloned.1.call-update) | async-done | bytes 65552 | tf_op jit(solution)/shard_map/psum | solution.py:171
  531.3 1.5 copy.33
  (109 shorter events, 23.9 us)
Async XLA Ops:
  7.2 43.4 %copy-start = (bf16[128,128]{1,0:T(8,128)(2,1)S(1)}, bf16[128,128]{1,0:T(8,128)(2,1)}, u32[]{:S(2)}) copy-start(bf16[128,128]{1,0:T(8,128)(2,1)} %param.29) | copy-start | bytes 98308
  7.2 17.2 %copy-start.1 = (bf16[512,128]{1,0:T(8,128)(2,1)S(1)}, bf16[512,128]{1,0:T(8,128)(2,1)}, u32[]{:S(2)}) copy-start(bf16[512,128]{1,0:T(8,128)(2,1)} %param.18) | copy-start | bytes 393220
  9.6 28.8 %collective-permute-start.1 = (bf16[1,128,128]{2,1,0:T(8,128)(2,1)S(1)}, bf16[1,128,128]{2,1,0:T(8,128)(2,1)S(1)}, u32[]{:S(2)}, u32[]{:S(2)}) collective-permute-start(bf16[1,128,128]{2,1,0:T(8,128)(2,1)S(1)} %get-tuple-element.9), channel_id=1, source_target_pairs={{8,0},{16,8},{24,16},{9,1},{17,9},{25,17},{10,2},{18,10},{26,18},{... | collective-permute-start | bytes 98312 | tf_op jit(solution)/shard_map/ppermute | solution.py:17
  10.9 27.5 %collective-permute-start = (bf16[1,128,128]{2,1,0:T(8,128)(2,1)S(1)}, bf16[1,128,128]{2,1,0:T(8,128)(2,1)S(1)}, u32[]{:S(2)}, u32[]{:S(2)}) collective-permute-start(bf16[1,128,128]{2,1,0:T(8,128)(2,1)S(1)} %get-tuple-element.8), channel_id=1, source_target_pairs={{0,8},{8,16},{16,24},{1,9},{9,17},{17,25},{2,10},{10,18},{18,26},{... | collective-permute-start | bytes 98312 | tf_op jit(solution)/shard_map/ppermute | solution.py:14
  18.6 19.8 %all-to-all-start = ((bf16[8,16,128]{2,1,0:T(8,128)(2,1)}), bf16[8,16,128]{2,1,0:T(8,128)(2,1)S(1)}, u32[]{:S(2)}, u32[]{:S(2)}) async-start(bf16[8,16,128]{2,1,0:T(8,128)(2,1)} %bitcast), calls=%async_computation | async-start | bytes 65536 | tf_op jit(solution)/shard_map/all_to_all | solution.py:105
  23.7 91.0 %reduce-scatter.3.cloned.1.call-start = ((), (), s32[]{:S(2)}) async-start(), calls=%async_computation.6 | async-start | bytes 147456 | tf_op jit(solution)/shard_map/reduce_scatter | solution.py:116
  24.4 12.2 %copy-start.4 = (bf16[128,128]{1,0:T(8,128)(2,1)S(1)}, bf16[128,128]{1,0:T(8,128)(2,1)}, u32[]{:S(2)}) copy-start(bf16[128,128]{1,0:T(8,128)(2,1)} %param.30) | copy-start | bytes 98308
  36.6 1.8 copy-start.14
  52.6 29.0 %copy-start.3 = (bf16[512,128]{1,0:T(8,128)(2,1)S(1)}, bf16[512,128]{1,0:T(8,128)(2,1)}, u32[]{:S(2)}) copy-start(bf16[512,128]{1,0:T(8,128)(2,1)} %param.19) | copy-start | bytes 393220
  76.4 78.8 %copy-start.5 = (bf16[128,128]{1,0:T(8,128)(2,1)S(1)}, bf16[128,128]{1,0:T(8,128)(2,1)}, u32[]{:S(2)}) copy-start(bf16[128,128]{1,0:T(8,128)(2,1)} %param.32) | copy-start | bytes 98308
  76.4 81.5 %copy-start.7 = (bf16[128,128]{1,0:T(8,128)(2,1)S(1)}, bf16[128,128]{1,0:T(8,128)(2,1)}, u32[]{:S(2)}) copy-start(bf16[128,128]{1,0:T(8,128)(2,1)} %param.34) | copy-start | bytes 98308
  81.5 70.4 %reduce-scatter.5.cloned.1.call-start = ((), (), s32[]{:S(2)}) async-start(), calls=%async_computation.7 | async-start | bytes 147456 | tf_op jit(solution)/shard_map/reduce_scatter | solution.py:117
  89.6 64.7 %copy-start.16 = (s32[1024]{0:T(1024)}, s32[1024]{0:T(1024)S(1)}, u32[]{:S(2)}) copy-start(s32[1024]{0:T(1024)S(1)} %pad_clamp_fusion.2) | copy-start | bytes 12292
  116.6 37.7 %all-to-all-start.1 = ((bf16[8,4,128]{2,1,0:T(4,128)(2,1)}), bf16[8,4,128]{2,1,0:T(4,128)(2,1)S(1)}, u32[]{:S(2)}, u32[]{:S(2)}) async-start(bf16[8,4,128]{2,1,0:T(4,128)(2,1)} %bitcast.7), calls=%async_computation.2 | async-start | bytes 16384 | tf_op jit(solution)/shard_map/all_to_all | solution.py:120
  121.0 167.7 %all-reduce.10.cloned.1.call-start = ((), (), s32[]{:S(2)}) async-start(), calls=%async_computation.9 | async-start | bytes 1048576 | tf_op jit(solution)/shard_map/psum | solution.py:129
  303.6 8.9 %copy-start.6 = (bf16[128,128]{1,0:T(8,128)(2,1)S(1)}, bf16[128,128]{1,0:T(8,128)(2,1)}, u32[]{:S(2)}) copy-start(bf16[128,128]{1,0:T(8,128)(2,1)} %param.32) | copy-start | bytes 98308
  305.2 9.0 %copy-start.11 = (f32[32,128]{1,0:T(8,128)S(1)}, f32[32,128]{1,0:T(8,128)}, u32[]{:S(2)}) copy-start(f32[32,128]{1,0:T(8,128)} %reduce-scatter.5.cloned.1.call-done) | copy-start | bytes 49156
  305.2 13.0 %copy-start.8 = (bf16[128,128]{1,0:T(8,128)(2,1)S(1)}, bf16[128,128]{1,0:T(8,128)(2,1)}, u32[]{:S(2)}) copy-start(bf16[128,128]{1,0:T(8,128)(2,1)} %param.33) | copy-start | bytes 98308
  305.2 13.2 %copy-start.17 = (s32[256]{0:T(256)S(1)}, s32[256]{0:T(256)}, u32[]{:S(2)}) copy-start(s32[256]{0:T(256)} %param.27) | copy-start | bytes 3076
  309.8 12.4 %copy-start.20 = (s32[32]{0:T(128)S(1)}, s32[32]{0:T(128)}, u32[]{:S(2)}) copy-start(s32[32]{0:T(128)} %fusion.45) | copy-start | bytes 388
  311.5 20.4 %copy-start.15 = (s32[1024]{0:T(1024)S(1)}, s32[1024]{0:T(1024)}, u32[]{:S(2)}) copy-start(s32[1024]{0:T(1024)} %pad_clamp_fusion) | copy-start | bytes 12292
  314.8 7.5 %all-to-all-start.2 = ((f32[8,4,128]{2,1,0:T(4,128)}), f32[8,4,128]{2,1,0:T(4,128)S(1)}, u32[]{:S(2)}, u32[]{:S(2)}) async-start(f32[8,4,128]{2,1,0:T(4,128)} %bitcast.10), calls=%async_computation.4 | async-start | bytes 32768 | tf_op jit(solution)/shard_map/all_to_all | solution.py:145
  318.4 15.1 %copy-start.9 = (bf16[128,128]{1,0:T(8,128)(2,1)S(1)}, bf16[128,128]{1,0:T(8,128)(2,1)}, u32[]{:S(2)}) copy-start(bf16[128,128]{1,0:T(8,128)(2,1)} %param.31) | copy-start | bytes 98308
  353.4 28.0 %copy-start.2 = (f32[512,128]{1,0:T(8,128)S(1)}, f32[512,128]{1,0:T(8,128)}, u32[]{:S(2)}) copy-start(f32[512,128]{1,0:T(8,128)} %gather_fusion.11) | copy-start | bytes 786436
  353.4 29.0 %copy-start.10 = (s32[4096]{0:T(1024)S(1)}, s32[4096]{0:T(1024)}, u32[]{:S(2)}) copy-start(s32[4096]{0:T(1024)} %param.23) | copy-start | bytes 49156
  378.0 32.3 %all-to-all-start.3 = ((f32[8,16,128]{2,1,0:T(8,128)}), f32[8,16,128]{2,1,0:T(8,128)S(1)}, u32[]{:S(2)}, u32[]{:S(2)}) async-start(f32[8,16,128]{2,1,0:T(8,128)} %bitcast.13), calls=%async_computation.5 | async-start | bytes 131072 | tf_op jit(solution)/shard_map/all_to_all | solution.py:159
  381.4 149.8 %all-reduce.8.cloned.1.call-start = ((), (), s32[]{:S(2)}) async-start(), calls=%async_computation.8 | async-start | bytes 131072 | tf_op jit(solution)/shard_map/psum | solution.py:171
  382.4 22.6 %copy-start.13 = (f32[1,128,128]{2,1,0:T(8,128)S(1)}, f32[1,128,128]{2,1,0:T(8,128)}, u32[]{:S(2)}) copy-start(f32[1,128,128]{2,1,0:T(8,128)} %get-tuple-element.6) | copy-start | bytes 196612
  382.4 23.9 %copy-start.12 = (f32[1,128,128]{2,1,0:T(8,128)S(1)}, f32[1,128,128]{2,1,0:T(8,128)}, u32[]{:S(2)}) copy-start(f32[1,128,128]{2,1,0:T(8,128)} %get-tuple-element.5) | copy-start | bytes 196612
  382.4 27.9 %copy-start.19 = (s32[128]{0:T(128)S(1)}, s32[128]{0:T(128)}, u32[]{:S(2)}) copy-start(s32[128]{0:T(128)} %fusion.46) | copy-start | bytes 1540
  382.4 29.2 %copy-start.18 = (pred[513]{0:T(1024)(128)(4,1)S(1)}, pred[513]{0:T(1024)(128)(4,1)}, u32[]{:S(2)}) copy-start(pred[513]{0:T(1024)(128)(4,1)} %constant.27.clone.1) | copy-start | bytes 1543
  405.0 6.8 %collective-permute-start.3 = (f32[1,128,128]{2,1,0:T(8,128)S(1)}, f32[1,128,128]{2,1,0:T(8,128)S(1)}, u32[]{:S(2)}, u32[]{:S(2)}) collective-permute-start(f32[1,128,128]{2,1,0:T(8,128)S(1)} %copy-done.13), channel_id=1, source_target_pairs={{8,0},{16,8},{24,16},{9,1},{17,9},{25,17},{10,2},{18,10},{26,18},{... | collective-permute-start | bytes 196616 | tf_op jit(solution)/shard_map/ppermute | solution.py:17
  406.3 5.5 %collective-permute-start.2 = (f32[1,128,128]{2,1,0:T(8,128)S(1)}, f32[1,128,128]{2,1,0:T(8,128)S(1)}, u32[]{:S(2)}, u32[]{:S(2)}) collective-permute-start(f32[1,128,128]{2,1,0:T(8,128)S(1)} %copy-done.12), channel_id=1, source_target_pairs={{0,8},{8,16},{16,24},{1,9},{9,17},{17,25},{2,10},{10,18},{18,26},{... | collective-permute-start | bytes 196616 | tf_op jit(solution)/shard_map/ppermute | solution.py:14
Sparse Core Ops, SparseCore 0:
  81.6 33.0 reduce-scatter.2
  118.3 33.5 reduce-scatter.4
  159.6 129.0 all-reduce.9
  410.4 120.7 all-reduce.7
where the time goes:
time: 541 us; the launch traced here: 539 us
  waiting for transfers between devices  299 us (55%)
  other arithmetic  105 us (19%)
  local copies, waits for them, and re-layouts  57.2 us (11%)
  starting transfers between devices  27.6 us (5%)
  blocking collectives  19.5 us (4%)
  matrix products  16.5 us (3%)
  between operations  14.3 us (3%)
    psum x1, waiting for transfers between devices, local(): top_total = lax.psum(top_partial, ('group', 'dom'))  127 us
    psum x1, waiting for transfers between devices, local(): grad_send = lax.psum(f_weight, ('group', 'dom'))  117 us
    reduce_scatter x1, waiting for transfers between devices, local(): lax.psum_scatter(grad_partial, 'dom', scatter_dimension=0, tiled=True)  30.2 us
    scatter-add x2, other arithmetic, edge_forward(): jax.ops.segment_sum(message.astype(jnp.float32), targets, num_segments=ow...  25.4 us
    scatter-add x2, other arithmetic, edge_backward(): jax.ops.segment_sum(jnp.dot(grad_pre, w_recv.T, preferred_element_type=jn...  24.4 us
    scatter-add x2, other arithmetic, edge_backward(): jax.ops.segment_sum(jnp.dot(grad_pre, w_send.T, preferred_element_type=jn...  24.3 us
    reduce_scatter x1, waiting for transfers between devices, local(): lax.psum_scatter(partial_value, 'dom', scatter_dimension=0, tiled=True)  23.3 us
    gather x2, local copies, waits for them, and re-layouts, edge_backward(): grad_pre = (grad_sum[targets] * silu_slope(preact)).astype(jnp.bfloat16)  15.8 us
  transfers between devices with their start and end apart: 12, of which 5 were waited for; matrix products, arithmetic and copies ran while one was open for 12% of the time, Pallas kernels for 0%

commit v1 on v0

--- a/solution.py
+++ b/solution.py
@@ -126,7 +126,7 @@
     )
     top_partial = jax.ops.segment_sum(coarse_mid.astype(jnp.float32), coarse_pool, num_segments=NCC)
     grad_top_partial = jax.ops.segment_sum(grad_coarse, coarse_pool, num_segments=NCC)
-    top_total = lax.psum(top_partial, ("group", "dom"))
+    top_total = jnp.sum(lax.all_gather(top_partial, ("group", "dom")), 0)
     grad_top = lax.psum(grad_top_partial, ("group", "dom"))
     pooled = 0.125 * top_total
     top_out, slope_in = top_forward(pooled, w_top)

time: 541 us -> 615 us (1.14)
  waiting for transfers between devices: 299 us -> 370 us
    all_gather x0 -> x1, waiting for transfers between devices: none -> 79.9 us  [local(): top_total = jnp.sum(lax.all_gather(top_partial, ('group', 'dom')), 0)]
    reduce_scatter x1, waiting for transfers between devices: 30.2 us -> 15.8 us  [local(): lax.psum_scatter(grad_partial, 'dom', scatter_dimension=0, tiled=True)]
    reduce_scatter x1, waiting for transfers between devices: 23.3 us -> 30 us  [local(): lax.psum_scatter(partial_value, 'dom', scatter_dimension=0, tiled=True)]
  transfers between devices with their start and end apart: 12 -> 13, of which waited for: 5 -> 7; matrix products, arithmetic and copies ran while one was open for 12% -> 13% of each run, Pallas kernels for 0% -> 0%
where the time goes in v1:
time: 615 us; the launch traced here: 613 us
  waiting for transfers between devices  370 us (60%)
  other arithmetic  109 us (18%)
  local copies, waits for them, and re-layouts  57.3 us (9%)
  starting transfers between devices  27.1 us (4%)
  blocking collectives  18.7 us (3%)
  matrix products  16.5 us (3%)
  between operations  14.3 us (2%)
    psum x1, waiting for transfers between devices, local(): grad_top = lax.psum(grad_top_partial, ('group', 'dom'))  123 us
    psum x1, waiting for transfers between devices, local(): grad_send = lax.psum(f_weight, ('group', 'dom'))  116 us
    all_gather x1, waiting for transfers between devices, local(): top_total = jnp.sum(lax.all_gather(top_partial, ('group', 'dom')), 0)  79.9 us
    reduce_scatter x1, waiting for transfers between devices, local(): lax.psum_scatter(partial_value, 'dom', scatter_dimension=0, tiled=True)  30 us
    scatter-add x2, other arithmetic, edge_forward(): jax.ops.segment_sum(message.astype(jnp.float32), targets, num_segments=ow...  25.4 us
    scatter-add x2, other arithmetic, edge_backward(): jax.ops.segment_sum(jnp.dot(grad_pre, w_recv.T, preferred_element_type=jn...  24.5 us
    scatter-add x2, other arithmetic, edge_backward(): jax.ops.segment_sum(jnp.dot(grad_pre, w_send.T, preferred_element_type=jn...  24.3 us
    reduce_scatter x1, waiting for transfers between devices, local(): lax.psum_scatter(grad_partial, 'dom', scatter_dimension=0, tiled=True)  15.8 us
  transfers between devices with their start and end apart: 13, of which 7 were waited for; matrix products, arithmetic and copies ran while one was open for 13% of the time, Pallas kernels for 0%

profile of v1, /device:TPU:1, one launch (start us, length us, event | category | flops | bytes accessed | tf_op | source)
XLA Modules:
  0.0 612.9 jit_solution(2472457165018205766)
XLA Ops:
  7.9 1.6 gather_fusion.1
  9.6 4.0 collective-permute-start
  13.6 1.3 collective-permute-start.1
  16.6 1.3 gather_fusion
  17.9 4.7 all-to-all-start
  23.3 12.1 %gather_fusion.3 = bf16[4096,128]{1,0:T(8,128)(2,1)S(1)} fusion(bf16[512,128]{1,0:T(8,128)(2,1)S(1)} %copy-done.1, s32[4096]{0:T(1024)S(1)} %fusion.37), kind=kCustom, calls=%fused_computation.3 | custom fusion | bytes 2113536 | tf_op jit(solution)/shard_map/gather | solution.py:29
  35.5 1.8 fusion.52
  37.3 12.1 %gather_fusion.2 = bf16[4096,128]{1,0:T(8,128)(2,1)S(1)} fusion(bf16[896,128]{1,0:T(8,128)(2,1)S(1)} %pad_maximum_fusion, s32[4096]{0:T(1024)S(1)} %fusion.36), kind=kCustom, calls=%fused_computation.2 | custom fusion | bytes 2113536 | tf_op jit(solution)/shard_map/gather | solution.py:28
  49.5 2.0 convolution_add_fusion
  51.5 23.8 %scatter_custom_fusion = f32[512,128]{1,0:T(8,128)} fusion(s32[4096]{0:T(1024)} %param.23, f32[4096,128]{1,0:T(8,128)S(1)} %convolution_add_fusion, f32[]{:T(128)} %constant.20.clone.1, f32[]{:T(128)} %constant.14.clone.1), kind=kCustom, calls=%fused_computation.28 | custom fusion | flops 3670016 | bytes 2360320 | tf_op jit(solution)/shard_map/scatter-add | solution.py:31
  75.3 1.8 fusion.3
  77.2 3.2 scatter_custom_fusion.1
  80.5 3.0 scatter_custom_fusion.4
  85.8 30.0 %reduce-scatter.3.cloned.1.call-done = f32[32,128]{1,0:T(8,128)} async-done(((f32[256,128]{1,0:T(8,128)}), f32[32,128]{1,0:T(8,128)}) %reduce-scatter.3.cloned.1.call-update) | async-done | bytes 16400 | tf_op jit(solution)/shard_map/reduce_scatter | solution.py:116
  117.7 4.5 all-to-all-start.1
  123.0 3.2 all-to-all-done.1
  127.3 1.6 scatter_custom_fusion.2
  129.1 1.5 scatter_custom_fusion.3
  136.5 15.8 %reduce-scatter.5.cloned.1.call-done = f32[32,128]{1,0:T(8,128)} async-done(((f32[256,128]{1,0:T(8,128)}), f32[32,128]{1,0:T(8,128)}) %reduce-scatter.5.cloned.1.call-update) | async-done | bytes 16400 | tf_op jit(solution)/shard_map/reduce_scatter | solution.py:117
  152.3 1.6 scatter_custom_fusion.5
  154.0 79.9 %all-gather.3.cloned.1.call-done = f32[16384,128]{1,0:T(8,128)} async-done(((f32[512,128]{1,0:T(8,128)}), f32[16384,128]{1,0:T(8,128)}) %all-gather.3.cloned.1.call-update) | async-done | bytes 8388624 | tf_op jit(solution)/shard_map/all_gather | solution.py:129
  233.8 4.5 reduce_sum.9
  238.3 2.0 add_convert_fusion.1
  240.3 122.9 %all-reduce.7.cloned.1.call-done = f32[512,128]{1,0:T(8,128)} async-done(((f32[512,128]{1,0:T(8,128)}), f32[512,128]{1,0:T(8,128)}) %all-reduce.7.cloned.1.call-update) | async-done | bytes 262160 | tf_op jit(solution)/shard_map/psum | solution.py:130
  363.2 2.0 convolution_add_fusion.1
  365.3 1.5 gather_fusion.9
  368.8 1.6 scatter_custom_fusion.6
  370.4 1.3 fusion.51
  371.7 5.1 all-to-all-start.2
  376.8 1.6 gather_fusion.7
  379.2 9.6 %all_gather.14 = bf16[256,128]{1,0:T(8,128)(2,1)S(1)} all-gather(bf16[32,128]{1,0:T(8,128)(2,1)S(1)} %add_convert_fusion.2), channel_id=1, replica_groups=mesh['group'=4,'dom'=8] {'dom'}, dimensions={0}, use_global_device_ids=true | all-gather | bytes 73728 | tf_op jit(solution)/shard_map/all_gather | solution.py:136
  388.8 1.5 gather_fusion.8
  390.2 1.6 add_convert_fusion
  392.8 2.1 scatter_fusion
  395.8 9.2 %all_gather.15 = f32[256,128]{1,0:T(8,128)S(1)} all-gather(f32[32,128]{1,0:T(8,128)S(1)} %slice.78), channel_id=1, replica_groups=mesh['group'=4,'dom'=8] {'dom'}, dimensions={0}, use_global_device_ids=true | all-gather | bytes 147456 | tf_op jit(solution)/shard_map/all_gather | solution.py:153
  405.0 1.8 gather_fusion.11
  407.9 14.1 %gather_fusion.12 = f32[4096,128]{1,0:T(8,128)} fusion(f32[512,128]{1,0:T(8,128)S(1)} %fusion.15, s32[4096]{0:T(1024)S(1)} %fusion.37), kind=kCustom, calls=%fused_computation.12 | custom fusion | bytes 4210688 | tf_op jit(solution)/shard_map/gather | solution.py:43
  422.0 2.4 multiply_convert_fusion
  424.4 1.8 fusion.56
  427.8 22.8 %scatter_custom_fusion.9 = f32[896,128]{1,0:T(8,128)S(1)} fusion(s32[4096]{0:T(1024)} %param.22, f32[4096,128]{1,0:T(8,128)} %fusion.56, f32[]{:T(128)} %constant.14.clone.1), kind=kCustom, calls=%fused_computation.54 | custom fusion | flops 524288 | bytes 459264 | tf_op jit(solution)/shard_map/scatter-add | solution.py:44
  451.2 3.4 all-to-all-start.3
  455.6 22.5 %scatter_fusion.2 = f32[512,128]{1,0:T(8,128)S(1)} fusion(f32[512,128]{1,0:T(8,128)S(1)} %slice_add_fusion, s32[4096]{0:T(1024)S(1)} %copy-done.10, f32[4096,128]{1,0:T(8,128)S(1)} %fusion.57), kind=kCustom, calls=%fused_computation.23 | custom fusion | flops 524288 | bytes 6307840 | tf_op jit(solution)/shard_map/scatter-add | solution.py:50
  478.2 2.7 collective-permute-start.2
  482.2 1.3 scatter_fusion.3
  483.7 2.2 collective-permute-done.3
  485.9 2.1 scatter_custom_fusion.12
  488.7 116.1 %all-reduce.9.cloned.1.call-done = f32[128,128]{1,0:T(8,128)} async-done(((f32[128,128]{1,0:T(8,128)}), f32[128,128]{1,0:T(8,128)}) %all-reduce.9.cloned.1.call-update) | async-done | bytes 65552 | tf_op jit(solution)/shard_map/psum | solution.py:171
  604.9 1.5 copy.32
  (113 shorter events, 26.6 us)
Async XLA Ops:
  7.2 42.3 %copy-start = (bf16[128,128]{1,0:T(8,128)(2,1)S(1)}, bf16[128,128]{1,0:T(8,128)(2,1)}, u32[]{:S(2)}) copy-start(bf16[128,128]{1,0:T(8,128)(2,1)} %param.29) | copy-start | bytes 98308
  7.2 16.1 %copy-start.1 = (bf16[512,128]{1,0:T(8,128)(2,1)S(1)}, bf16[512,128]{1,0:T(8,128)(2,1)}, u32[]{:S(2)}) copy-start(bf16[512,128]{1,0:T(8,128)(2,1)} %param.18) | copy-start | bytes 393220
  9.6 27.7 %collective-permute-start = (bf16[1,128,128]{2,1,0:T(8,128)(2,1)S(1)}, bf16[1,128,128]{2,1,0:T(8,128)(2,1)S(1)}, u32[]{:S(2)}, u32[]{:S(2)}) collective-permute-start(bf16[1,128,128]{2,1,0:T(8,128)(2,1)S(1)} %get-tuple-element.6), channel_id=1, source_target_pairs={{0,8},{8,16},{16,24},{1,9},{9,17},{17,25},{2,10},{10,18},{18,26},{... | collective-permute-start | bytes 98312 | tf_op jit(solution)/shard_map/ppermute | solution.py:14
  13.6 23.7 %collective-permute-start.1 = (bf16[1,128,128]{2,1,0:T(8,128)(2,1)S(1)}, bf16[1,128,128]{2,1,0:T(8,128)(2,1)S(1)}, u32[]{:S(2)}, u32[]{:S(2)}) collective-permute-start(bf16[1,128,128]{2,1,0:T(8,128)(2,1)S(1)} %get-tuple-element.7), channel_id=1, source_target_pairs={{8,0},{16,8},{24,16},{9,1},{17,9},{25,17},{10,2},{18,10},{26,18},{... | collective-permute-start | bytes 98312 | tf_op jit(solution)/shard_map/ppermute | solution.py:17
  17.9 19.4 %all-to-all-start = ((bf16[8,16,128]{2,1,0:T(8,128)(2,1)}), bf16[8,16,128]{2,1,0:T(8,128)(2,1)S(1)}, u32[]{:S(2)}, u32[]{:S(2)}) async-start(bf16[8,16,128]{2,1,0:T(8,128)(2,1)} %bitcast), calls=%async_computation | async-start | bytes 65536 | tf_op jit(solution)/shard_map/all_to_all | solution.py:105
  22.6 93.1 %reduce-scatter.3.cloned.1.call-start = ((), (), s32[]{:S(2)}) async-start(), calls=%async_computation.6 | async-start | bytes 147456 | tf_op jit(solution)/shard_map/reduce_scatter | solution.py:116
  23.3 12.2 %copy-start.4 = (bf16[128,128]{1,0:T(8,128)(2,1)S(1)}, bf16[128,128]{1,0:T(8,128)(2,1)}, u32[]{:S(2)}) copy-start(bf16[128,128]{1,0:T(8,128)(2,1)} %param.30) | copy-start | bytes 98308
  35.5 1.8 copy-start.15
  51.5 29.0 %copy-start.3 = (bf16[512,128]{1,0:T(8,128)(2,1)S(1)}, bf16[512,128]{1,0:T(8,128)(2,1)}, u32[]{:S(2)}) copy-start(bf16[512,128]{1,0:T(8,128)(2,1)} %param.19) | copy-start | bytes 393220
  51.5 75.5 %copy-start.6 = (bf16[128,128]{1,0:T(8,128)(2,1)S(1)}, bf16[128,128]{1,0:T(8,128)(2,1)}, u32[]{:S(2)}) copy-start(bf16[128,128]{1,0:T(8,128)(2,1)} %param.32) | copy-start | bytes 98308
  51.5 75.6 %copy-start.8 = (bf16[128,128]{1,0:T(8,128)(2,1)S(1)}, bf16[128,128]{1,0:T(8,128)(2,1)}, u32[]{:S(2)}) copy-start(bf16[128,128]{1,0:T(8,128)(2,1)} %param.33) | copy-start | bytes 98308
  75.3 53.6 %copy-start.7 = (bf16[128,128]{1,0:T(8,128)(2,1)S(1)}, bf16[128,128]{1,0:T(8,128)(2,1)}, u32[]{:S(2)}) copy-start(bf16[128,128]{1,0:T(8,128)(2,1)} %param.34) | copy-start | bytes 98308
  80.5 71.9 %reduce-scatter.5.cloned.1.call-start = ((), (), s32[]{:S(2)}) async-start(), calls=%async_computation.7 | async-start | bytes 147456 | tf_op jit(solution)/shard_map/reduce_scatter | solution.py:117
  117.7 8.5 %all-to-all-start.1 = ((bf16[8,4,128]{2,1,0:T(4,128)(2,1)}), bf16[8,4,128]{2,1,0:T(4,128)(2,1)S(1)}, u32[]{:S(2)}, u32[]{:S(2)}) async-start(bf16[8,4,128]{2,1,0:T(4,128)(2,1)} %bitcast.7), calls=%async_computation.2 | async-start | bytes 16384 | tf_op jit(solution)/shard_map/all_to_all | solution.py:120
  122.1 111.7 %all-gather.3.cloned.1.call-start = ((), (), s32[]{:S(2)}) async-start(), calls=%async_computation.10 | async-start | bytes 8650752 | tf_op jit(solution)/shard_map/all_gather | solution.py:129
  122.1 116.2 %copy-start.16 = (s32[1024]{0:T(1024)}, s32[1024]{0:T(1024)S(1)}, u32[]{:S(2)}) copy-start(s32[1024]{0:T(1024)S(1)} %pad_clamp_fusion.2) | copy-start | bytes 12292
  129.1 109.3 %copy-start.12 = (f32[32,128]{1,0:T(8,128)}, f32[32,128]{1,0:T(8,128)S(1)}, u32[]{:S(2)}) copy-start(f32[32,128]{1,0:T(8,128)S(1)} %fusion.5) | copy-start | bytes 49156
  130.6 232.6 %all-reduce.7.cloned.1.call-start = ((), (), s32[]{:S(2)}) async-start(), calls=%async_computation.8 | async-start | bytes 524288 | tf_op jit(solution)/shard_map/psum | solution.py:130
  132.9 232.3 %copy-start.17 = (s32[1024]{0:T(1024)}, s32[1024]{0:T(1024)S(1)}, u32[]{:S(2)}) copy-start(s32[1024]{0:T(1024)S(1)} %pad_clamp_fusion.1) | copy-start | bytes 12292
  233.8 4.5 copy-start.20
  238.3 128.5 %copy-start.11 = (f32[32,128]{1,0:T(8,128)S(1)}, f32[32,128]{1,0:T(8,128)}, u32[]{:S(2)}) copy-start(f32[32,128]{1,0:T(8,128)} %reduce-scatter.5.cloned.1.call-done) | copy-start | bytes 49156
  371.7 23.2 %all-to-all-start.2 = ((f32[8,4,128]{2,1,0:T(4,128)}), f32[8,4,128]{2,1,0:T(4,128)S(1)}, u32[]{:S(2)}, u32[]{:S(2)}) async-start(f32[8,4,128]{2,1,0:T(4,128)} %bitcast.11), calls=%async_computation.4 | async-start | bytes 32768 | tf_op jit(solution)/shard_map/all_to_all | solution.py:145
  392.8 14.0 %copy-start.9 = (bf16[128,128]{1,0:T(8,128)(2,1)S(1)}, bf16[128,128]{1,0:T(8,128)(2,1)}, u32[]{:S(2)}) copy-start(bf16[128,128]{1,0:T(8,128)(2,1)} %param.31) | copy-start | bytes 98308
  424.4 1.8 copy-start.5
  426.6 28.0 %copy-start.2 = (f32[512,128]{1,0:T(8,128)S(1)}, f32[512,128]{1,0:T(8,128)}, u32[]{:S(2)}) copy-start(f32[512,128]{1,0:T(8,128)} %gather_fusion.11) | copy-start | bytes 786436
  426.6 28.9 %copy-start.10 = (s32[4096]{0:T(1024)S(1)}, s32[4096]{0:T(1024)}, u32[]{:S(2)}) copy-start(s32[4096]{0:T(1024)} %param.23) | copy-start | bytes 49156
  451.2 31.0 %all-to-all-start.3 = ((f32[8,16,128]{2,1,0:T(8,128)}), f32[8,16,128]{2,1,0:T(8,128)S(1)}, u32[]{:S(2)}, u32[]{:S(2)}) async-start(f32[8,16,128]{2,1,0:T(8,128)} %bitcast.14), calls=%async_computation.5 | async-start | bytes 131072 | tf_op jit(solution)/shard_map/all_to_all | solution.py:159
  454.6 150.3 %all-reduce.9.cloned.1.call-start = ((), (), s32[]{:S(2)}) async-start(), calls=%async_computation.9 | async-start | bytes 131072 | tf_op jit(solution)/shard_map/psum | solution.py:171
  455.6 22.6 %copy-start.14 = (f32[1,128,128]{2,1,0:T(8,128)S(1)}, f32[1,128,128]{2,1,0:T(8,128)}, u32[]{:S(2)}) copy-start(f32[1,128,128]{2,1,0:T(8,128)} %get-tuple-element.3) | copy-start | bytes 196612
  455.6 25.3 %copy-start.13 = (f32[1,128,128]{2,1,0:T(8,128)S(1)}, f32[1,128,128]{2,1,0:T(8,128)}, u32[]{:S(2)}) copy-start(f32[1,128,128]{2,1,0:T(8,128)} %get-tuple-element.4) | copy-start | bytes 196612
  455.6 26.6 %copy-start.19 = (s32[128]{0:T(128)S(1)}, s32[128]{0:T(128)}, u32[]{:S(2)}) copy-start(s32[128]{0:T(128)} %fusion.46) | copy-start | bytes 1540
  455.6 27.9 %copy-start.18 = (pred[513]{0:T(1024)(128)(4,1)S(1)}, pred[513]{0:T(1024)(128)(4,1)}, u32[]{:S(2)}) copy-start(pred[513]{0:T(1024)(128)(4,1)} %constant.27.clone.1) | copy-start | bytes 1543
  478.2 5.6 collective-permute-start.2
  480.9 5.0 collective-permute-start.3
Sparse Core Ops, SparseCore 0:
  80.6 35.1 reduce-scatter.2
  118.7 33.5 reduce-scatter.4
  155.8 77.9 all-gather.2
  239.2 123.9 all-reduce.6
  482.3 122.5 all-reduce.8
